TPU v7x, 32 devices: a whole 2x2x4 slice. The times are simulated.
32 devices in a mesh: dp: 4 (over y, x), fsdp: 8 (over z, core).
Axes of the slice: x: 2, y: 2, z: 4, core: 2. Of those that a mesh axis runs over, the one named last changes fastest.
Arguments:
- inputs: bfloat16 [4, 16, 3584], P('dp', 'fsdp'), may hold values from -16 to 16
- baseline: bfloat16 [4, 16, 3584], P('dp', 'fsdp'), may hold values from -6 to 6
- cotangent: bfloat16 [4, 16, 3584], P('dp', 'fsdp'), may hold values from -6 to 6
- interval: int32 [4], P('dp'), may hold values from 0 to 7
- pre_gain: float32 [3584], replicated, may hold values from 0.1 to 1.9
- post_gain: float32 [3584], replicated, may hold values from 0.1 to 1.9
- gate_weight: bfloat16 [3584, 14336], P('dp', 'fsdp'), may hold values from -0.09375 to 0.09375
- up_weight: bfloat16 [3584, 14336], P('dp', 'fsdp'), may hold values from -0.09375 to 0.09375
- down_weight: bfloat16 [14336, 3584], P('fsdp', 'dp'), may hold values from -0.046875 to 0.046875
Outputs:
- attribution: float32 [4, 16, 3584], P('dp', 'fsdp')
All inputs are finite; a program needn't handle non-finite values.
Results may differ from a plain program's by a relative error of at most 0.0027.
Values may be sent and summed in bfloat16 or wider, within the bound.
No kernel may reach another device: no remote copies, remote signals or barrier semaphores. Data moves between devices by JAX's collectives and lax.ppermute only.
A program may use at most 128 MiB of HBM per device.

v0:
```python
import math
import jax
import jax.numpy as jnp
from jax import lax
from jax.sharding import PartitionSpec as P

STEPS = 4
TOTAL = 32
epsilon = 1e-06
root_coef = math.sqrt(2.0 / math.pi)


def gelu_parts(argument):
    tangent = jnp.tanh(root_coef * (argument + 0.044715 * argument * argument * argument))
    gelu_value = 0.5 * argument * (1.0 + tangent)
    gelu_slope = 0.5 * (1.0 + tangent) + 0.5 * argument * (1.0 - tangent * tangent) * root_coef * (
        1.0 + 3.0 * 0.044715 * argument * argument
    )
    return (gelu_value, gelu_slope)


def norm_back(grad_in, source, gain):
    scaled = grad_in * gain
    inverse = lax.rsqrt(jnp.mean(source * source, axis=-1, keepdims=True) + epsilon)
    inner_mean = jnp.mean(scaled * source, axis=-1, keepdims=True)
    return inverse * (scaled - source * inverse * inverse * inner_mean)


def per_device(
    inputs, baseline, cotangent, interval, pre_gain, post_gain, gate_weight, up_weight, down_weight
):
    gate_full, up_full = (
        lax.all_gather(gate_weight, "dp", axis=0, tiled=True),
        lax.all_gather(up_weight, "dp", axis=0, tiled=True),
    )
    down_full = lax.all_gather(down_weight, "dp", axis=1, tiled=True)
    own_rows = inputs.shape[1]
    model_width = inputs.shape[2]
    whole_in, whole_base, whole_target = (
        lax.all_gather(inputs, "fsdp", axis=1, tiled=True),
        lax.all_gather(baseline, "fsdp", axis=1, tiled=True),
        lax.all_gather(cotangent, "fsdp", axis=1, tiled=True),
    )
    target_all = whole_target[0].astype(jnp.float32)
    source = whole_in[0].astype(jnp.float32)
    anchor = whole_base[0].astype(jnp.float32)
    offset = source - anchor
    own_source = inputs[0].astype(jnp.float32)
    own_anchor = baseline[0].astype(jnp.float32)
    own_offset = own_source - own_anchor
    summed = jnp.zeros((own_rows, model_width), jnp.float32)
    for step_index in range(STEPS):
        fraction = (interval[0].astype(jnp.float32) * STEPS + (step_index + 0.5)) / TOTAL
        sample_point = anchor + fraction * offset
        inverse = lax.rsqrt(jnp.mean(sample_point * sample_point, axis=-1, keepdims=True) + epsilon)
        normed = (sample_point * inverse * pre_gain).astype(jnp.bfloat16)
        gate_val = jnp.dot(normed, gate_full, preferred_element_type=jnp.float32)
        up_val = jnp.dot(normed, up_full, preferred_element_type=jnp.float32)
        gelu_value, gelu_slope = gelu_parts(gate_val)
        hidden = (gelu_value * up_val).astype(jnp.bfloat16)
        branch = lax.psum(jnp.dot(hidden, down_full, preferred_element_type=jnp.float32), "fsdp")
        branch_grad = norm_back(target_all, branch, post_gain).astype(jnp.bfloat16)
        hidden_grad = jnp.dot(branch_grad, down_full.T, preferred_element_type=jnp.float32)
        gate_grad = (hidden_grad * up_val * gelu_slope).astype(jnp.bfloat16)
        up_grad = (hidden_grad * gelu_value).astype(jnp.bfloat16)
        normed_grad = lax.psum_scatter(
            jnp.dot(gate_grad, gate_full.T, preferred_element_type=jnp.float32)
            + jnp.dot(up_grad, up_full.T, preferred_element_type=jnp.float32),
            "fsdp",
            scatter_dimension=0,
            tiled=True,
        )
        own_point = own_anchor + fraction * own_offset
        summed = summed + norm_back(normed_grad, own_point, pre_gain)
    return (own_offset * summed / STEPS)[None]


def solution(mesh):
    return jax.shard_map(
        per_device,
        mesh=mesh,
        in_specs=(
            P("dp", "fsdp", None),
            P("dp", "fsdp", None),
            P("dp", "fsdp", None),
            P("dp"),
            P(),
            P(),
            P("dp", "fsdp"),
            P("dp", "fsdp"),
            P("fsdp", "dp"),
        ),
        out_specs=P("dp", "fsdp", None),
        check_vma=False,
    )
```

profile of v0, /device:TPU:0, one launch (start us, length us, event | category | flops | bytes accessed | tf_op | source)
XLA Modules:
  0.0 617.1 jit_solution(8745663518771204632)
XLA Ops:
  10.2 16.0 %all_gather.18 = bf16[1,16,3584]{2,0,1:T(2,128)(2,1)S(1)} all-gather(bf16[1,2,3584]{2,0,1:T(2,128)(2,1)S(1)} %copy.10), channel_id=1, replica_groups=mesh['dp'=4,'fsdp'=8] {'fsdp'}, dimensions={1}, use_global_device_ids=true | all-gather | bytes 129024 | tf_op jit(solution)/shard_map/all_gather | solution.py:41
  27.1 14.1 %all_gather.19 = bf16[1,16,3584]{2,0,1:T(2,128)(2,1)S(1)} all-gather(bf16[1,2,3584]{2,0,1:T(2,128)(2,1)S(1)} %copy.11), channel_id=1, replica_groups=mesh['dp'=4,'fsdp'=8] {'fsdp'}, dimensions={1}, use_global_device_ids=true | all-gather | bytes 129024 | tf_op jit(solution)/shard_map/all_gather | solution.py:40
  42.4 94.1 %all-gather.4.cloned.1.call-done = bf16[3584,1792]{1,0:T(8,128)(2,1)} async-done(((bf16[896,1792]{1,0:T(8,128)(2,1)}), bf16[3584,1792]{1,0:T(8,128)(2,1)}) %all-gather.4.cloned.1.call-update) | async-done | bytes 12845072 | tf_op jit(solution)/shard_map/all_gather | solution.py:33
  136.5 6.4 %fusion.162 = f32[16,1792]{1,0:T(8,128)S(1)} fusion(bf16[16,3584]{1,0:T(8,128)(2,1)S(1)} %get-tuple-element.35, bf16[3584,1792]{1,0:T(8,128)(2,1)} %all-gather.4.cloned.1.call-done), kind=kOutput, calls=%fused_computation.234 | convolution fusion | flops 205520896 | bytes 13074432 | tf_op jit(solution)/shard_map/dot_general | solution.py:57
  142.9 120.0 %all-gather.6.cloned.1.call-done = bf16[3584,1792]{1,0:T(8,128)(2,1)} async-done(((bf16[896,1792]{1,0:T(8,128)(2,1)}), bf16[3584,1792]{1,0:T(8,128)(2,1)}) %all-gather.6.cloned.1.call-update) | async-done | bytes 12845072 | tf_op jit(solution)/shard_map/all_gather | solution.py:34
  262.9 6.6 %fusion.163 = f32[16,1792]{1,0:T(8,128)S(1)} fusion(bf16[16,3584]{1,0:T(8,128)(2,1)S(1)} %get-tuple-element.35, bf16[3584,1792]{1,0:T(8,128)(2,1)} %all-gather.6.cloned.1.call-done), kind=kOutput, calls=%fused_computation.235 | convolution fusion | flops 205520896 | bytes 13074432 | tf_op jit(solution)/shard_map/dot_general | solution.py:58
  269.5 8.6 %fusion.160 = f32[16,1792]{1,0:T(8,128)S(1)} fusion(bf16[16,3584]{1,0:T(8,128)(2,1)S(1)} %get-tuple-element.37, bf16[3584,1792]{1,0:T(8,128)(2,1)} %all-gather.4.cloned.1.call-done), kind=kOutput, calls=%fused_computation.232 | convolution fusion | flops 205520896 | bytes 13074432 | tf_op jit(solution)/shard_map/dot_general | solution.py:57
  278.2 1.8 fusion.161
  284.1 1.8 fusion.159
  285.9 1.8 fusion.157
  287.6 13.2 %fusion.156 = f32[16,1792]{1,0:T(8,128)S(1)} fusion(bf16[16,3584]{1,0:T(8,128)(2,1)S(1)} %get-tuple-element.38, bf16[3584,1792]{1,0:T(8,128)(2,1)S(1)} %bitcast.186), kind=kOutput, calls=%fused_computation.228 | convolution fusion | flops 205520896 | bytes 13074432 | tf_op jit(solution)/shard_map/dot_general | solution.py:57
  300.8 88.6 %all-gather.8.cloned.1.call-done = bf16[1792,3584]{1,0:T(8,128)(2,1)} async-done(((bf16[1792,896]{1,0:T(8,128)(2,1)}), bf16[1792,3584]{1,0:T(8,128)(2,1)}) %all-gather.8.cloned.1.call-update) | async-done | bytes 12845072 | tf_op jit(solution)/shard_map/all_gather | solution.py:36
  389.4 7.3 %fusion.75 = f32[16,3584]{1,0:T(8,128)} fusion(bf16[1792,3584]{1,0:T(8,128)(2,1)} %all-gather.8.cloned.1.call-done, f32[16,1792]{1,0:T(8,128)S(1)} %fusion.163, f32[16,1792]{1,0:T(8,128)S(1)} %fusion.162), kind=kOutput, calls=%fused_computation.113 | convolution fusion | flops 205807616 | bytes 13303808 | tf_op jit(solution)/shard_map/dot_general | solution.py:61
  397.8 2.5 fusion.74
  400.2 2.5 fusion.73
  402.7 2.5 fusion.72
  405.3 14.3 %all_gather.23 = bf16[1,16,3584]{2,0,1:T(2,128)(2,1)S(1)} all-gather(bf16[1,2,3584]{2,0,1:T(2,128)(2,1)S(1)} %copy.13), channel_id=1, replica_groups=mesh['dp'=4,'fsdp'=8] {'fsdp'}, dimensions={1}, use_global_device_ids=true | all-gather | bytes 129024 | tf_op jit(solution)/shard_map/all_gather | solution.py:42
  419.6 44.6 %all-reduce.11.cloned.1.call-done = (f32[16,3584]{1,0:T(8,128)}, f32[16,3584]{1,0:T(8,128)}, f32[16,3584]{1,0:T(8,128)}, f32[16,3584]{1,0:T(8,128)}) async-done(((f32[16,3584]{1,0:T(8,128)}, f32[16,3584]{1,0:T(8,128)}, f32[16,3584]{1,0:T(8,128)}, f32[16,3584]{1,0:T(8,128)}), (f32[16,3584]{1,0:T(8,128)}, f32[16,3584]{1,0:T(8,128)}, f32[16,3584]{1,0:T(8,128)}, ...) | async-done | bytes 917520 | tf_op jit(solution)/shard_map/psum | solution.py:61
  466.9 8.3 %fusion.48 = f32[16,1792]{1,0:T(8,128)S(1)} fusion(bf16[1792,3584]{1,0:T(8,128)(2,1)} %all-gather.8.cloned.1.call-done, f32[16,3584]{1,0:T(8,128)} %get-tuple-element.32, bf16[1,16,3584]{2,1,0:T(8,128)(2,1)S(1)} %get-tuple-element.33, f32[16]{0:T(128)S(1)} %broadcast_multiply_fusion, f32[16]{0:T(128)S(1)} %add_rsqrt_fusion, f32[3584]{0:T(1024)S(1)} %copy-done.4), kind=kOutput, calls=%fused_computation.78 | convolution fusion | flops 205979648 | bytes 13318272 | tf_op jit(solution)/shard_map/dot_general | solution.py:63
  475.2 8.2 %fusion.76 = f32[16,3584]{1,0:T(8,128)S(1)} fusion(bf16[3584,1792]{1,0:T(8,128)(2,1)} %all-gather.4.cloned.1.call-done, f32[16,1792]{1,0:T(8,128)S(1)} %fusion.162, f32[16,1792]{1,0:T(8,128)S(1)} %fusion.48, f32[16,1792]{1,0:T(8,128)S(1)} %fusion.163), kind=kOutput, calls=%fused_computation.114 | convolution fusion | flops 206094336 | bytes 13418496 | tf_op jit(solution)/shard_map/dot_general | solution.py:67
  483.5 4.1 convolution_add_fusion
  487.6 8.1 %fusion.50 = f32[16,1792]{1,0:T(8,128)S(1)} fusion(bf16[1792,3584]{1,0:T(8,128)(2,1)} %all-gather.8.cloned.1.call-done, f32[16,3584]{1,0:T(8,128)S(1)} %copy-done.3, bf16[1,16,3584]{2,1,0:T(8,128)(2,1)S(1)} %get-tuple-element.33, f32[16]{0:T(128)S(1)} %broadcast_multiply_fusion.1, f32[16]{0:T(128)S(1)} %add_rsqrt_fusion.3, f32[3584]{0:T(1024)S(1)} %copy-done.4), kind=kOutput, calls=%fused_computation.79 | convolution fusion | flops 205979648 | bytes 13318272 | tf_op jit(solution)/shard_map/dot_general | solution.py:63
  495.7 8.1 %fusion.78 = f32[16,3584]{1,0:T(8,128)S(1)} fusion(bf16[3584,1792]{1,0:T(8,128)(2,1)} %all-gather.4.cloned.1.call-done, f32[16,1792]{1,0:T(8,128)S(1)} %fusion.160, f32[16,1792]{1,0:T(8,128)S(1)} %fusion.50, f32[16,1792]{1,0:T(8,128)S(1)} %fusion.161), kind=kOutput, calls=%fused_computation.115 | convolution fusion | flops 206094336 | bytes 13418496 | tf_op jit(solution)/shard_map/dot_general | solution.py:67
  503.8 4.2 convolution_add_fusion.1
  508.0 8.1 %fusion.52 = f32[16,1792]{1,0:T(8,128)S(1)} fusion(bf16[1792,3584]{1,0:T(8,128)(2,1)} %all-gather.8.cloned.1.call-done, f32[16,3584]{1,0:T(8,128)S(1)} %copy-done.2, bf16[1,16,3584]{2,1,0:T(8,128)(2,1)S(1)} %get-tuple-element.33, f32[16]{0:T(128)S(1)} %broadcast_multiply_fusion.2, f32[16]{0:T(128)S(1)} %add_rsqrt_fusion.6, f32[3584]{0:T(1024)S(1)} %copy-done.4), kind=kOutput, calls=%fused_computation.80 | convolution fusion | flops 205979648 | bytes 13318272 | tf_op jit(solution)/shard_map/dot_general | solution.py:63
  516.0 8.3 %fusion.80 = f32[16,3584]{1,0:T(8,128)S(1)} fusion(bf16[3584,1792]{1,0:T(8,128)(2,1)} %all-gather.4.cloned.1.call-done, f32[16,1792]{1,0:T(8,128)S(1)} %fusion.158, f32[16,1792]{1,0:T(8,128)S(1)} %fusion.52, f32[16,1792]{1,0:T(8,128)S(1)} %fusion.159), kind=kOutput, calls=%fused_computation.116 | convolution fusion | flops 206094336 | bytes 13418496 | tf_op jit(solution)/shard_map/dot_general | solution.py:67
  524.3 4.1 convolution_add_fusion.2
  528.5 8.1 %fusion.54 = f32[16,1792]{1,0:T(8,128)S(1)} fusion(bf16[1792,3584]{1,0:T(8,128)(2,1)} %all-gather.8.cloned.1.call-done, f32[16,3584]{1,0:T(8,128)S(1)} %copy-done.1, bf16[1,16,3584]{2,1,0:T(8,128)(2,1)S(1)} %get-tuple-element.33, f32[16]{0:T(128)S(1)} %broadcast_multiply_fusion.3, f32[3584]{0:T(1024)S(1)} %copy-done.4, f32[16]{0:T(128)S(1)} %add_rsqrt_fusion.9), kind=kOutput, calls=%fused_computation.81 | convolution fusion | flops 205979648 | bytes 13318272 | tf_op jit(solution)/shard_map/dot_general | solution.py:63
  536.6 8.1 %fusion.82 = f32[16,3584]{1,0:T(8,128)S(1)} fusion(bf16[3584,1792]{1,0:T(8,128)(2,1)} %all-gather.4.cloned.1.call-done, f32[16,1792]{1,0:T(8,128)S(1)} %fusion.156, f32[16,1792]{1,0:T(8,128)S(1)} %fusion.54, f32[16,1792]{1,0:T(8,128)S(1)} %fusion.157), kind=kOutput, calls=%fused_computation.117 | convolution fusion | flops 206094336 | bytes 13418496 | tf_op jit(solution)/shard_map/dot_general | solution.py:67
  544.7 4.1 convolution_add_fusion.3
  550.1 56.7 %all-reduce.9.cloned.1.call-done = (f32[16,3584]{1,0:T(8,128)}, f32[16,3584]{1,0:T(8,128)}, f32[16,3584]{1,0:T(8,128)}, f32[16,3584]{1,0:T(8,128)}) async-done(((f32[16,3584]{1,0:T(8,128)}, f32[16,3584]{1,0:T(8,128)}, f32[16,3584]{1,0:T(8,128)}, f32[16,3584]{1,0:T(8,128)}), (f32[16,3584]{1,0:T(8,128)}, f32[16,3584]{1,0:T(8,128)}, f32[16,3584]{1,0:T(8,128)}, ...) | async-done | bytes 917520
  608.3 1.9 multiply_bitcast_fusion
  (86 shorter events, 15.2 us)
Async XLA Ops:
  6.5 130.0 %all-gather.4.cloned.1.call-start = ((), (), s32[]{:S(2)}) async-start(), calls=%async_computation | async-start | bytes 16056320 | tf_op jit(solution)/shard_map/all_gather | solution.py:33
  7.3 255.7 %all-gather.6.cloned.1.call-start = ((), (), s32[]{:S(2)}) async-start(), calls=%async_computation.1 | async-start | bytes 16056320 | tf_op jit(solution)/shard_map/all_gather | solution.py:34
  8.0 381.4 %all-gather.8.cloned.1.call-start = ((), (), s32[]{:S(2)}) async-start(), calls=%async_computation.2 | async-start | bytes 16056320 | tf_op jit(solution)/shard_map/all_gather | solution.py:36
  8.7 455.5 %all-reduce.11.cloned.1.call-start = ((), (), s32[]{:S(2)}) async-start(), calls=%async_computation.4 | async-start | bytes 1835008 | tf_op jit(solution)/shard_map/psum | solution.py:61
  262.9 15.2 %slice-start = ((s8[12845056]{0:T(1024)(128)(4,1)}), s8[4194304]{0:T(1024)(128)(4,1)S(1)}, s32[]{:S(2)}) async-start(s8[12845056]{0:T(1024)(128)(4,1)} %bitcast.181), calls=%async_computation.5 | async-start | bytes 8388608
  262.9 15.2 %slice-start.1 = ((s8[12845056]{0:T(1024)(128)(4,1)}), s8[4194304]{0:T(1024)(128)(4,1)S(1)}, s32[]{:S(2)}) async-start(s8[12845056]{0:T(1024)(128)(4,1)} %bitcast.181), calls=%async_computation.6 | async-start | bytes 8388608
  269.5 8.6 %slice-start.2 = ((s8[12845056]{0:T(1024)(128)(4,1)}), s8[4194304]{0:T(1024)(128)(4,1)S(1)}, s32[]{:S(2)}) async-start(s8[12845056]{0:T(1024)(128)(4,1)} %bitcast.181), calls=%async_computation.7 | async-start | bytes 8388608
  269.5 8.7 %slice-start.3 = ((s8[12845056]{0:T(1024)(128)(4,1)}), s8[262144]{0:T(1024)(128)(4,1)S(1)}, s32[]{:S(2)}) async-start(s8[12845056]{0:T(1024)(128)(4,1)} %bitcast.181), calls=%async_computation.8 | async-start | bytes 524288
  269.5 10.5 %slice-start.8 = ((s8[12845056]{0:T(1024)(128)(4,1)}), s8[4194304]{0:T(1024)(128)(4,1)S(1)}, s32[]{:S(2)}) async-start(s8[12845056]{0:T(1024)(128)(4,1)} %bitcast.185), calls=%async_computation.13 | async-start | bytes 8388608
  269.5 11.7 %slice-start.9 = ((s8[12845056]{0:T(1024)(128)(4,1)}), s8[4194304]{0:T(1024)(128)(4,1)S(1)}, s32[]{:S(2)}) async-start(s8[12845056]{0:T(1024)(128)(4,1)} %bitcast.185), calls=%async_computation.14 | async-start | bytes 8388608
  278.2 4.2 slice-start.10
  278.2 4.2 slice-start.11
  389.4 8.4 %copy-start = (bf16[1792,3584]{1,0:T(8,128)(2,1)S(1)}, bf16[1792,3584]{1,0:T(8,128)(2,1)}, u32[]{:S(2)}) copy-start(bf16[1792,3584]{1,0:T(8,128)(2,1)} %all-gather.8.cloned.1.call-done) | copy-start | bytes 38535172
  402.7 2.5 copy-start.8
  402.7 61.5 %copy-start.4 = (f32[3584]{0:T(1024)S(1)}, f32[3584]{0:T(1024)}, u32[]{:S(2)}) copy-start(f32[3584]{0:T(1024)} %param.14) | copy-start | bytes 43012
  405.1 78.3 %slice-start.4 = ((s8[12845056]{0:T(1024)(128)(4,1)}), s8[262144]{0:T(1024)(128)(4,1)S(1)}, s32[]{:S(2)}) async-start(s8[12845056]{0:T(1024)(128)(4,1)} %bitcast.183), calls=%async_computation.9 | async-start | bytes 524288
  405.2 201.6 %all-reduce.9.cloned.1.call-start = ((), (), s32[]{:S(2)}) async-start(), calls=%async_computation.3 | async-start | bytes 1835008
  466.9 16.6 %slice-start.5 = ((s8[12845056]{0:T(1024)(128)(4,1)}), s8[4194304]{0:T(1024)(128)(4,1)S(1)}, s32[]{:S(2)}) async-start(s8[12845056]{0:T(1024)(128)(4,1)} %bitcast.183), calls=%async_computation.10 | async-start | bytes 8388608
  466.9 16.6 %slice-start.6 = ((s8[12845056]{0:T(1024)(128)(4,1)}), s8[4194304]{0:T(1024)(128)(4,1)S(1)}, s32[]{:S(2)}) async-start(s8[12845056]{0:T(1024)(128)(4,1)} %bitcast.183), calls=%async_computation.11 | async-start | bytes 8388608
  475.2 8.3 %slice-start.7 = ((s8[12845056]{0:T(1024)(128)(4,1)}), s8[4194304]{0:T(1024)(128)(4,1)S(1)}, s32[]{:S(2)}) async-start(s8[12845056]{0:T(1024)(128)(4,1)} %bitcast.183), calls=%async_computation.12 | async-start | bytes 8388608
  475.2 12.4 %copy-start.3 = (f32[16,3584]{1,0:T(8,128)S(1)}, f32[16,3584]{1,0:T(8,128)}, u32[]{:S(2)}) copy-start(f32[16,3584]{1,0:T(8,128)} %get-tuple-element.31) | copy-start | bytes 688132
  495.7 12.3 %copy-start.2 = (f32[16,3584]{1,0:T(8,128)S(1)}, f32[16,3584]{1,0:T(8,128)}, u32[]{:S(2)}) copy-start(f32[16,3584]{1,0:T(8,128)} %get-tuple-element.30) | copy-start | bytes 688132
  516.0 12.4 %copy-start.1 = (f32[16,3584]{1,0:T(8,128)S(1)}, f32[16,3584]{1,0:T(8,128)}, u32[]{:S(2)}) copy-start(f32[16,3584]{1,0:T(8,128)} %get-tuple-element.29) | copy-start | bytes 688132
  536.5 12.3 %copy-start.9 = (u32[32]{0:T(128)S(1)}, u32[32]{0:T(128)}, u32[]{:S(2)}) copy-start(u32[32]{0:T(128)} %constant.72) | copy-start | bytes 388
  536.5 70.2 %copy-start.5 = (f32[3584]{0:T(1024)S(1)}, f32[3584]{0:T(1024)}, u32[]{:S(2)}) copy-start(f32[3584]{0:T(1024)} %param.13) | copy-start | bytes 43012
  536.5 70.2 %copy-start.6 = (bf16[1,2,3584]{2,1,0:T(2,128)(2,1)S(1)}, bf16[1,2,3584]{2,1,0:T(2,128)(2,1)}, u32[]{:S(2)}) copy-start(bf16[1,2,3584]{2,1,0:T(2,128)(2,1)} %param.10) | copy-start | bytes 43012
  536.6 70.2 %copy-start.7 = (bf16[1,2,3584]{2,1,0:T(2,128)(2,1)S(1)}, bf16[1,2,3584]{2,1,0:T(2,128)(2,1)}, u32[]{:S(2)}) copy-start(bf16[1,2,3584]{2,1,0:T(2,128)(2,1)} %param.9) | copy-start | bytes 43012
Sparse Core Ops, SparseCore 0:
  9.2 127.2 all-gather.3
  138.3 124.5 all-gather.5
  264.8 124.5 all-gather.7
  405.3 58.8 all-reduce.10
  549.0 57.7 all-reduce.8
where the time goes:
time: 627 us; the launch traced here: 617 us
  waiting for transfers between devices  406 us (65%)
  matrix products  138 us (22%)
  blocking collectives  44.4 us (7%)
  between operations  15.1 us (2%)
  other arithmetic  7.36 us (1%)
    all_gather x1, waiting for transfers between devices, per_device(): lax.all_gather(up_weight, 'dp', axis=0, tiled=True)  120 us
    all_gather x1, waiting for transfers between devices, per_device(): lax.all_gather(gate_weight, 'dp', axis=0, tiled=True)  94.1 us
    all_gather x1, waiting for transfers between devices, per_device(): down_full = lax.all_gather(down_weight, 'dp', axis=1, tiled=True)  88.6 us
    unnamed x6, waiting for transfers between devices  58.8 us
    psum x1, waiting for transfers between devices, per_device(): lax.psum(jnp.dot(hidden, down_full, preferred_element_type=jnp.float32),...  44.6 us
    dot_general x4, matrix products, per_device(): jnp.dot(gate_grad, gate_full.T, preferred_element_type=jnp.float32)  32.7 us
    dot_general x4, matrix products, per_device(): jnp.dot(branch_grad, down_full.T, preferred_element_type=jnp.float32)  32.5 us
    dot_general x4, matrix products, per_device(): gate_val = jnp.dot(normed, gate_full, preferred_element_type=jnp.float32)  30 us
  transfers between devices with their start and end apart: 5, of which 5 were waited for; matrix products, arithmetic and copies ran while one was open for 7% of the time, Pallas kernels for 0%

commit v1 on v0

--- a/solution.py
+++ b/solution.py
@@ -1,3 +1,4 @@
+import functools
 import math
 import jax
 import jax.numpy as jnp
@@ -8,6 +9,14 @@
 TOTAL = 32
 epsilon = 1e-06
 root_coef = math.sqrt(2.0 / math.pi)
+
+
+def draft_bench(obj, mesh_dim):
+    small = jnp.concatenate(jax.lax.all_gather(obj, axis_name=mesh_dim), axis=1)
+    return small
+
+
+list_results_up = functools.partial(draft_bench, mesh_dim="dp")
 
 
 def gelu_parts(argument):
@@ -33,7 +42,7 @@
         lax.all_gather(gate_weight, "dp", axis=0, tiled=True),
         lax.all_gather(up_weight, "dp", axis=0, tiled=True),
     )
-    down_full = lax.all_gather(down_weight, "dp", axis=1, tiled=True)
+    down_full = list_results_up(down_weight)
     own_rows = inputs.shape[1]
     model_width = inputs.shape[2]
     whole_in, whole_base, whole_target = (

time: 627 us -> 665 us (1.061)
  waiting for transfers between devices: 406 us -> 425 us
  local copies, waits for them, and re-layouts: 5.67 us -> 22.8 us
  matrix products: 138 us -> 147 us
    reshape x0 -> x1, local copies, waits for them, and re-layouts: none -> 18.9 us  [draft_bench(): small = jnp.concatenate(jax.lax.all_gather(obj, axis_name=mesh_dim), axis=1)]
    dot_general x4, matrix products: 32.5 us -> 17 us  [per_device(): jnp.dot(branch_grad, down_full.T, preferred_element_type=jnp.float32)]
    dot_general x4, matrix products: 11.9 us -> 25.8 us  [per_device(): up_val = jnp.dot(normed, up_full, preferred_element_type=jnp.float32)]
    dot_general x4, matrix products: 14.7 us -> 28.4 us  [per_device(): jnp.dot(hidden, down_full, preferred_element_type=jnp.float32)]
    all_gather x1, waiting for transfers between devices: 94.1 us -> 108 us  [per_device(): lax.all_gather(gate_weight, 'dp', axis=0, tiled=True)]
  transfers between devices with their start and end apart: 5 -> 5, of which waited for: 5 -> 5; matrix products, arithmetic and copies ran while one was open for 7% -> 4% of each run, Pallas kernels for 0% -> 0%
where the time goes in v1:
time: 665 us; the launch traced here: 661 us
  waiting for transfers between devices  425 us (64%)
  matrix products  147 us (22%)
  blocking collectives  44.4 us (7%)
  local copies, waits for them, and re-layouts  22.8 us (3%)
  between operations  15 us (2%)
  other arithmetic  7.39 us (1%)
    all_gather x1, waiting for transfers between devices, per_device(): lax.all_gather(up_weight, 'dp', axis=0, tiled=True)  120 us
    all_gather x1, waiting for transfers between devices, per_device(): lax.all_gather(gate_weight, 'dp', axis=0, tiled=True)  108 us
    all_gather x1, waiting for transfers between devices, draft_bench(): small = jnp.concatenate(jax.lax.all_gather(obj, axis_name=mesh_dim), axis=1)  94.1 us
    unnamed x6, waiting for transfers between devices  58.8 us
    psum x1, waiting for transfers between devices, per_device(): lax.psum(jnp.dot(hidden, down_full, preferred_element_type=jnp.float32),...  44.5 us
    dot_general x4, matrix products, per_device(): jnp.dot(gate_grad, gate_full.T, preferred_element_type=jnp.float32)  33.1 us
    dot_general x4, matrix products, per_device(): jnp.dot(hidden, down_full, preferred_element_type=jnp.float32)  28.4 us
    dot_general x4, matrix products, per_device(): up_val = jnp.dot(normed, up_full, preferred_element_type=jnp.float32)  25.8 us
  transfers between devices with their start and end apart: 5, of which 5 were waited for; matrix products, arithmetic and copies ran while one was open for 4% of the time, Pallas kernels for 0%

profile of v1, /device:TPU:0, one launch (start us, length us, event | category | flops | bytes accessed | tf_op | source)
XLA Modules:
  0.0 661.3 jit_solution(13318239830308574954)
XLA Ops:
  10.2 16.0 %all_gather.21 = bf16[1,16,3584]{2,0,1:T(2,128)(2,1)S(1)} all-gather(bf16[1,2,3584]{2,0,1:T(2,128)(2,1)S(1)} %copy.11), channel_id=1, replica_groups=mesh['dp'=4,'fsdp'=8] {'fsdp'}, dimensions={1}, use_global_device_ids=true | all-gather | bytes 129024 | tf_op jit(solution)/shard_map/all_gather | solution.py:50
  27.1 14.1 %all_gather.22 = bf16[1,16,3584]{2,0,1:T(2,128)(2,1)S(1)} all-gather(bf16[1,2,3584]{2,0,1:T(2,128)(2,1)S(1)} %copy.12), channel_id=1, replica_groups=mesh['dp'=4,'fsdp'=8] {'fsdp'}, dimensions={1}, use_global_device_ids=true | all-gather | bytes 129024 | tf_op jit(solution)/shard_map/all_gather | solution.py:49
  42.4 94.1 %all-gather.9.cloned.1.call-done = bf16[7168,896]{1,0:T(8,128)(2,1)} async-done(((bf16[1792,896]{1,0:T(8,128)(2,1)}), bf16[7168,896]{1,0:T(8,128)(2,1)}) %all-gather.9.cloned.1.call-update) | async-done | bytes 12845072 | tf_op jit(solution)/shard_map/all_gather | solution.py:15
  136.5 18.9 %copy.14 = bf16[1792,4,896]{0,2,1:T(8,128)(2,1)} copy(bf16[1792,4,896]{2,0,1:T(8,128)(2,1)} %bitcast.197) | data formatting | bytes 25690112 | tf_op jit(solution)/shard_map/reshape | solution.py:15
  155.4 107.5 %all-gather.5.cloned.1.call-done = bf16[3584,1792]{1,0:T(8,128)(2,1)} async-done(((bf16[896,1792]{1,0:T(8,128)(2,1)}), bf16[3584,1792]{1,0:T(8,128)(2,1)}) %all-gather.5.cloned.1.call-update) | async-done | bytes 12845072 | tf_op jit(solution)/shard_map/all_gather | solution.py:42
  262.9 6.4 fusion.156
  269.3 120.0 %all-gather.7.cloned.1.call-done = bf16[3584,1792]{1,0:T(8,128)(2,1)} async-done(((bf16[896,1792]{1,0:T(8,128)(2,1)}), bf16[3584,1792]{1,0:T(8,128)(2,1)}) %all-gather.7.cloned.1.call-update) | async-done | bytes 12845072 | tf_op jit(solution)/shard_map/all_gather | solution.py:43
  389.4 6.6 fusion.157
  397.7 4.1 fusion.72
  401.8 6.4 fusion.159
  408.2 6.4 fusion.158
  414.6 4.1 fusion.73
  418.7 6.4 fusion.161
  425.1 6.4 fusion.160
  431.6 16.0 %fusion.74 = f32[16,3584]{1,0:T(8,128)} fusion(bf16[1792,3584]{0,1:T(8,128)(2,1)S(1)} %bitcast.189, f32[16,1792]{1,0:T(8,128)S(1)} %fusion.161, f32[16,1792]{1,0:T(8,128)S(1)} %fusion.160), kind=kOutput, calls=%fused_computation.112 | convolution fusion | flops 205807616 | bytes 13303808 | tf_op jit(solution)/shard_map/dot_general | solution.py:70
  447.6 6.4 fusion.163
  454.0 6.4 fusion.162
  460.4 4.1 fusion.75
  464.7 14.3 %all_gather.27 = bf16[1,16,3584]{2,0,1:T(2,128)(2,1)S(1)} all-gather(bf16[1,2,3584]{2,0,1:T(2,128)(2,1)S(1)} %copy.15), channel_id=1, replica_groups=mesh['dp'=4,'fsdp'=8] {'fsdp'}, dimensions={1}, use_global_device_ids=true | all-gather | bytes 129024 | tf_op jit(solution)/shard_map/all_gather | solution.py:51
  479.0 44.5 %all-reduce.11.cloned.1.call-done = (f32[16,3584]{1,0:T(8,128)}, f32[16,3584]{1,0:T(8,128)}, f32[16,3584]{1,0:T(8,128)}, f32[16,3584]{1,0:T(8,128)}) async-done(((f32[16,3584]{1,0:T(8,128)}, f32[16,3584]{1,0:T(8,128)}, f32[16,3584]{1,0:T(8,128)}, f32[16,3584]{1,0:T(8,128)}), (f32[16,3584]{1,0:T(8,128)}, f32[16,3584]{1,0:T(8,128)}, f32[16,3584]{1,0:T(8,128)}, ...) | async-done | bytes 917520 | tf_op jit(solution)/shard_map/psum | solution.py:70
  526.2 6.7 %fusion.54 = f32[16,1792]{1,0:T(8,128)S(1)} fusion(bf16[1792,3584]{0,1:T(8,128)(2,1)} %bitcast.185, f32[16,3584]{1,0:T(8,128)} %get-tuple-element.29, bf16[1,16,3584]{2,1,0:T(8,128)(2,1)S(1)} %get-tuple-element.33, f32[16]{0:T(128)S(1)} %broadcast_multiply_fusion.3, f32[3584]{0:T(1024)S(1)} %copy-done.1, f32[16]{0:T(128)S(1)} %add_rsqrt_fusion.9), kind=kOutput, calls=%fused_computation.81 | convolution fusion | flops 205979648 | bytes 13318272 | tf_op jit(solution)/shard_map/dot_general | solution.py:72
  533.0 6.6 fusion.52
  543.3 8.8 %fusion.82 = f32[16,3584]{1,0:T(8,128)S(1)} fusion(bf16[3584,1792]{1,0:T(8,128)(2,1)} %all-gather.5.cloned.1.call-done, f32[16,1792]{1,0:T(8,128)S(1)} %fusion.156, f32[16,1792]{1,0:T(8,128)S(1)} %fusion.54, f32[16,1792]{1,0:T(8,128)S(1)} %fusion.157), kind=kOutput, calls=%fused_computation.117 | convolution fusion | flops 206094336 | bytes 13418496 | tf_op jit(solution)/shard_map/dot_general | solution.py:76
  552.2 4.1 convolution_add_fusion.3
  556.3 8.1 %fusion.80 = f32[16,3584]{1,0:T(8,128)S(1)} fusion(bf16[3584,1792]{1,0:T(8,128)(2,1)} %all-gather.5.cloned.1.call-done, f32[16,1792]{1,0:T(8,128)S(1)} %fusion.158, f32[16,1792]{1,0:T(8,128)S(1)} %fusion.52, f32[16,1792]{1,0:T(8,128)S(1)} %fusion.159), kind=kOutput, calls=%fused_computation.116 | convolution fusion | flops 206094336 | bytes 13418496 | tf_op jit(solution)/shard_map/dot_general | solution.py:76
  564.4 4.3 convolution_add_fusion.2
  568.7 8.1 %fusion.78 = f32[16,3584]{1,0:T(8,128)S(1)} fusion(bf16[3584,1792]{1,0:T(8,128)(2,1)} %all-gather.5.cloned.1.call-done, f32[16,1792]{1,0:T(8,128)S(1)} %fusion.160, f32[16,1792]{1,0:T(8,128)S(1)} %fusion.50, f32[16,1792]{1,0:T(8,128)S(1)} %fusion.161), kind=kOutput, calls=%fused_computation.115 | convolution fusion | flops 206094336 | bytes 13418496 | tf_op jit(solution)/shard_map/dot_general | solution.py:76
  576.7 4.2 convolution_add_fusion.1
  580.9 8.1 %fusion.76 = f32[16,3584]{1,0:T(8,128)S(1)} fusion(bf16[3584,1792]{1,0:T(8,128)(2,1)} %all-gather.5.cloned.1.call-done, f32[16,1792]{1,0:T(8,128)S(1)} %fusion.162, f32[16,1792]{1,0:T(8,128)S(1)} %fusion.48, f32[16,1792]{1,0:T(8,128)S(1)} %fusion.163), kind=kOutput, calls=%fused_computation.114 | convolution fusion | flops 206094336 | bytes 13418496 | tf_op jit(solution)/shard_map/dot_general | solution.py:76
  589.0 4.1 convolution_add_fusion
  594.4 56.7 %all-reduce.9.cloned.1.call-done = (f32[16,3584]{1,0:T(8,128)}, f32[16,3584]{1,0:T(8,128)}, f32[16,3584]{1,0:T(8,128)}, f32[16,3584]{1,0:T(8,128)}) async-done(((f32[16,3584]{1,0:T(8,128)}, f32[16,3584]{1,0:T(8,128)}, f32[16,3584]{1,0:T(8,128)}, f32[16,3584]{1,0:T(8,128)}), (f32[16,3584]{1,0:T(8,128)}, f32[16,3584]{1,0:T(8,128)}, f32[16,3584]{1,0:T(8,128)}, ...) | async-done | bytes 917520
  652.7 1.9 multiply_bitcast_fusion
  (78 shorter events, 15.3 us)
Async XLA Ops:
  6.5 130.0 %all-gather.9.cloned.1.call-start = ((), (), s32[]{:S(2)}) async-start(), calls=%async_computation.2 | async-start | bytes 16056320 | tf_op jit(solution)/shard_map/all_gather | solution.py:15
  7.3 255.7 %all-gather.5.cloned.1.call-start = ((), (), s32[]{:S(2)}) async-start(), calls=%async_computation | async-start | bytes 16056320 | tf_op jit(solution)/shard_map/all_gather | solution.py:42
  8.0 381.4 %all-gather.7.cloned.1.call-start = ((), (), s32[]{:S(2)}) async-start(), calls=%async_computation.1 | async-start | bytes 16056320 | tf_op jit(solution)/shard_map/all_gather | solution.py:43
  8.7 514.8 %all-reduce.11.cloned.1.call-start = ((), (), s32[]{:S(2)}) async-start(), calls=%async_computation.4 | async-start | bytes 1835008 | tf_op jit(solution)/shard_map/psum | solution.py:70
  389.4 8.3 %copy-start = (bf16[1792,4,896]{0,2,1:T(8,128)(2,1)S(1)}, bf16[1792,4,896]{0,2,1:T(8,128)(2,1)}, u32[]{:S(2)}) copy-start(bf16[1792,4,896]{0,2,1:T(8,128)(2,1)} %copy.14) | copy-start | bytes 38535172
  454.0 10.7 %copy-start.8 = (bf16[1,2,3584]{2,1,0:T(2,128)(2,1)S(1)}, bf16[1,2,3584]{2,1,0:T(2,128)(2,1)}, u32[]{:S(2)}) copy-start(bf16[1,2,3584]{2,1,0:T(2,128)(2,1)} %param.11) | copy-start | bytes 43012
  454.0 69.5 %copy-start.1 = (f32[3584]{0:T(1024)S(1)}, f32[3584]{0:T(1024)}, u32[]{:S(2)}) copy-start(f32[3584]{0:T(1024)} %param.14) | copy-start | bytes 43012
  464.6 186.5 %all-reduce.9.cloned.1.call-start = ((), (), s32[]{:S(2)}) async-start(), calls=%async_computation.3 | async-start | bytes 1835008
  523.5 9.4 %copy-start.4 = (f32[16,3584]{1,0:T(8,128)S(1)}, f32[16,3584]{1,0:T(8,128)}, u32[]{:S(2)}) copy-start(f32[16,3584]{1,0:T(8,128)} %get-tuple-element.30) | copy-start | bytes 688132
  526.2 13.4 %slice-start = ((s8[12845056]{0:T(1024)(128)(4,1)}), s8[4194304]{0:T(1024)(128)(4,1)S(1)}, s32[]{:S(2)}) async-start(s8[12845056]{0:T(1024)(128)(4,1)} %bitcast.191), calls=%async_computation.5 | async-start | bytes 8388608
  526.2 13.4 %slice-start.1 = ((s8[12845056]{0:T(1024)(128)(4,1)}), s8[4194304]{0:T(1024)(128)(4,1)S(1)}, s32[]{:S(2)}) async-start(s8[12845056]{0:T(1024)(128)(4,1)} %bitcast.191), calls=%async_computation.6 | async-start | bytes 8388608
  532.9 6.6 %slice-start.2 = ((s8[12845056]{0:T(1024)(128)(4,1)}), s8[4194304]{0:T(1024)(128)(4,1)S(1)}, s32[]{:S(2)}) async-start(s8[12845056]{0:T(1024)(128)(4,1)} %bitcast.191), calls=%async_computation.7 | async-start | bytes 8388608
  532.9 6.7 %slice-start.3 = ((s8[12845056]{0:T(1024)(128)(4,1)}), s8[262144]{0:T(1024)(128)(4,1)S(1)}, s32[]{:S(2)}) async-start(s8[12845056]{0:T(1024)(128)(4,1)} %bitcast.191), calls=%async_computation.8 | async-start | bytes 524288
  533.0 6.7 %copy-start.3 = (f32[16,3584]{1,0:T(8,128)S(1)}, f32[16,3584]{1,0:T(8,128)}, u32[]{:S(2)}) copy-start(f32[16,3584]{1,0:T(8,128)} %get-tuple-element.31) | copy-start | bytes 688132
  539.6 1.8 copy-start.2
  541.5 10.7 %slice-start.4 = ((s8[12845056]{0:T(1024)(128)(4,1)}), s8[4194304]{0:T(1024)(128)(4,1)S(1)}, s32[]{:S(2)}) async-start(s8[12845056]{0:T(1024)(128)(4,1)} %bitcast.195), calls=%async_computation.9 | async-start | bytes 8388608
  541.5 10.7 %slice-start.5 = ((s8[12845056]{0:T(1024)(128)(4,1)}), s8[4194304]{0:T(1024)(128)(4,1)S(1)}, s32[]{:S(2)}) async-start(s8[12845056]{0:T(1024)(128)(4,1)} %bitcast.195), calls=%async_computation.10 | async-start | bytes 8388608
  541.5 10.7 %slice-start.6 = ((s8[12845056]{0:T(1024)(128)(4,1)}), s8[4194304]{0:T(1024)(128)(4,1)S(1)}, s32[]{:S(2)}) async-start(s8[12845056]{0:T(1024)(128)(4,1)} %bitcast.195), calls=%async_computation.11 | async-start | bytes 8388608
  543.3 8.9 %slice-start.7 = ((s8[12845056]{0:T(1024)(128)(4,1)}), s8[262144]{0:T(1024)(128)(4,1)S(1)}, s32[]{:S(2)}) async-start(s8[12845056]{0:T(1024)(128)(4,1)} %bitcast.195), calls=%async_computation.12 | async-start | bytes 524288
  580.9 12.3 %copy-start.9 = (u32[32]{0:T(128)S(1)}, u32[32]{0:T(128)}, u32[]{:S(2)}) copy-start(u32[32]{0:T(128)} %constant.72) | copy-start | bytes 388
  580.9 70.2 %copy-start.5 = (f32[3584]{0:T(1024)S(1)}, f32[3584]{0:T(1024)}, u32[]{:S(2)}) copy-start(f32[3584]{0:T(1024)} %param.13) | copy-start | bytes 43012
  580.9 70.2 %copy-start.6 = (bf16[1,2,3584]{2,1,0:T(2,128)(2,1)S(1)}, bf16[1,2,3584]{2,1,0:T(2,128)(2,1)}, u32[]{:S(2)}) copy-start(bf16[1,2,3584]{2,1,0:T(2,128)(2,1)} %param.10) | copy-start | bytes 43012
  580.9 70.2 %copy-start.7 = (bf16[1,2,3584]{2,1,0:T(2,128)(2,1)S(1)}, bf16[1,2,3584]{2,1,0:T(2,128)(2,1)}, u32[]{:S(2)}) copy-start(bf16[1,2,3584]{2,1,0:T(2,128)(2,1)} %param.9) | copy-start | bytes 43012
Sparse Core Ops, SparseCore 0:
  9.2 127.2 all-gather.8
  138.3 124.5 all-gather.4
  264.8 124.5 all-gather.6
  464.7 58.7 all-reduce.10
  593.3 57.7 all-reduce.8
